TPU v7x, 32 devices: a whole 2x2x4 slice. The times are simulated.
32 devices in a mesh: span: 32 (over z, y, x, core).
Axes of the slice: x: 2, y: 2, z: 4, core: 2. Of those that a mesh axis runs over, the one named last changes fastest.
Arguments:
- returns: bfloat16 [256, 262144], P(None, 'span'), may hold values from -40 to 40
- market: bfloat16 [262144], P('span'), may hold values from -12 to 12
- mask: int32 [262144], P('span'), may hold values 0 or 1
- counts: int32 [32], P('span'), may hold values from 0 to 8192, as said below
Outputs:
- slope: float32 [256, 131072], P(None, 'span')
Inputs may be any that keep to these rules, and one draw needn't show every extreme that they name: For every span d, the counts of spans 0 to d sum to between (d + 1) * 4096 and (d + 2) * 4096; all counts sum to exactly 131072; some span holds exactly 8192.
All inputs are finite; a program needn't handle non-finite values. No bound on the sum of `mask` on one device may be relied on, other than what follows from the above.
Results may differ from a plain program's by a relative error of at most 0.00039.
Values may be sent and summed in bfloat16 or wider, within the bound.
A program may use at most 64 MiB of HBM per device.

v0:
```python
import jax
import jax.numpy as jnp
from jax import lax
from jax.sharding import PartitionSpec as P

WIN = 1024
BLOCK = 512
QROWS = 4096


RIDGE = 0.1


def shifted(value, axis, steps):
    count = lax.axis_size(axis)
    initial, last = (max(0, -steps), min(count, count - steps))
    return lax.ppermute(value, axis, [(source, source + steps) for source in range(initial, last)])


def band_matrix():
    row_index = jnp.arange(BLOCK + WIN, dtype=jnp.int32)[:, None]
    col_index = jnp.arange(BLOCK, dtype=jnp.int32)[None, :]
    inside = (row_index >= col_index + 1) & (row_index <= col_index + WIN)
    return inside.astype(jnp.bfloat16)


def stacked(y_values, x_values, w_values):
    cross_terms = (x_values.astype(jnp.float32)[None, :] * y_values.astype(jnp.float32)).astype(
        jnp.bfloat16
    )
    square = (x_values.astype(jnp.float32) * x_values.astype(jnp.float32)).astype(jnp.bfloat16)
    return jnp.concatenate(
        [cross_terms, y_values, w_values[None, :], x_values[None, :], square[None, :]], 0
    )


def slopes_of(moments):
    stocks = (moments.shape[0] - 3) // 2
    sum_xy = moments[:stocks]
    sum_y = moments[stocks : 2 * stocks]
    sum_w = moments[2 * stocks]
    sum_x = moments[2 * stocks + 1]
    sum_xx = moments[2 * stocks + 2]
    numerator = sum_w * sum_xy - sum_x * sum_y
    denominator = sum_w * sum_xx - sum_x * sum_x + RIDGE * WIN * WIN
    return numerator / denominator


def per_device(returns, market, mask, counts):
    quota = QROWS
    my_index = lax.axis_index("span")
    own_count = counts[0]
    gathered = lax.all_gather(counts, "span", axis=0, tiled=True)
    earlier = jnp.arange(gathered.shape[0], dtype=jnp.int32) < my_index
    before = jnp.sum(jnp.where(earlier, gathered, 0))
    capacity = returns.shape[1]
    row_index = jnp.arange(capacity, dtype=jnp.int32)
    weight = jnp.where(row_index < own_count, mask, 0).astype(jnp.float32)
    y_values = (returns.astype(jnp.float32) * weight[None, :]).astype(jnp.bfloat16)
    x_values = (market.astype(jnp.float32) * weight).astype(jnp.bfloat16)
    combined = jnp.concatenate(
        [y_values, x_values[None, :], weight.astype(jnp.bfloat16)[None, :]], 0
    )
    padded = jnp.pad(combined, ((0, 0), (quota, 0)))
    shift_base = my_index * quota - before

    def take_rows(first, length):
        return lax.dynamic_slice_in_dim(padded, first + quota, length, 1)

    own_rows = take_rows(shift_base, quota)
    incoming = shifted(take_rows(shift_base + quota, quota), "span", 1)
    window = own_rows + incoming
    halo_rows = shifted(window[:, quota - WIN :], "span", 1)
    extended = jnp.concatenate([halo_rows, window], 1)
    stocks = extended.shape[0] - 2
    stacked_rows = stacked(extended[:stocks], extended[stocks], extended[stocks + 1])
    band_ones = band_matrix()

    def one_block(block_index):
        window_piece = lax.dynamic_slice_in_dim(stacked_rows, block_index * BLOCK, BLOCK + WIN, 1)
        return slopes_of(jnp.dot(window_piece, band_ones, preferred_element_type=jnp.float32))

    blocks = lax.map(one_block, jnp.arange(quota // BLOCK, dtype=jnp.int32))
    return jnp.transpose(blocks, (1, 0, 2)).reshape(stocks, quota)


def solution(mesh):
    return jax.shard_map(
        per_device,
        mesh=mesh,
        in_specs=(P(None, "span"), P("span"), P("span"), P("span")),
        out_specs=P(None, "span"),
        check_vma=False,
    )
```

profile of v0, /device:TPU:8, one launch (start us, length us, event | category | flops | bytes accessed | tf_op | source)
XLA Modules:
  0.0 172.2 jit_solution(4214599199169973241)
XLA Ops:
  0.7 0.1 dynamic-update-slice
  0.8 40.4 %all-reduce.1 = s32[32]{0:T(128)S(1)} all-reduce(s32[32]{0:T(128)S(1)} %dynamic-update-slice), channel_id=1, replica_groups=mesh['span'=32] {'span'}, use_global_device_ids=true, to_apply=%add.1 | all-reduce | flops 32 | bytes 256
  41.2 0.7 fusion.22
  42.5 0.8 multiply_convert_fusion.2
  43.3 5.2 %multiply_convert_fusion = bf16[256,8192]{1,0:T(8,128)(2,1)} fusion(bf16[256,8192]{1,0:T(8,128)(2,1)} %param.6, f32[8192]{0:T(1024)S(1)} %get-tuple-element.66), kind=kLoop, calls=%fused_computation.23 | loop fusion | flops 6291456 | bytes 8421376 | tf_op jit(solution)/shard_map/convert_element_type | solution.py:59
  48.5 3.9 %fusion.20 = bf16[258,12288]{1,0:T(8,128)(2,1)S(1)} fusion(bf16[1,8192]{1,0:T(2,128)(2,1)S(1)} %broadcast_in_dim.30, bf16[1,8192]{1,0:T(2,128)(2,1)S(1)} %broadcast_in_dim.29, bf16[256,8192]{1,0:T(8,128)(2,1)} %multiply_convert_fusion), kind=kLoop, calls=%fused_computation.25 | loop fusion | flops 31703040 | bytes 10567680 | tf_op jit(solution)/shard_map/concatenate | solution.py:61
  52.4 0.0 copy-start
  52.4 2.7 %copy-done = bf16[258,12288]{1,0:T(8,128)(2,1)} copy-done((bf16[258,12288]{1,0:T(8,128)(2,1)}, bf16[258,12288]{1,0:T(8,128)(2,1)S(1)}, u32[]{:S(2)}) %copy-start) | copy-done | bytes 6340632
  55.1 0.9 constant_dynamic-slice_fusion
  56.0 1.9 %collective-permute-start = (bf16[258,4096]{1,0:T(8,128)(2,1)S(1)}, bf16[258,4096]{1,0:T(8,128)(2,1)}, u32[]{:S(2)}, u32[]{:S(2)}) collective-permute-start(bf16[258,4096]{1,0:T(8,128)(2,1)S(1)} %constant_dynamic-slice_fusion), channel_id=1, source_target_pairs={{0,1},{1,2},{2,3},{3,4},{4,5},{5,6},{6,7},{7,8},{8,9},{9,10},{10,1... | collective-permute-start | bytes 6340616 | tf_op jit(solution)/shard_map/ppermute | solution.py:17
  57.9 28.0 %collective-permute-done = bf16[258,4096]{1,0:T(8,128)(2,1)} collective-permute-done((bf16[258,4096]{1,0:T(8,128)(2,1)S(1)}, bf16[258,4096]{1,0:T(8,128)(2,1)}, u32[]{:S(2)}, u32[]{:S(2)}) %collective-permute-start) | collective-permute-done | bytes 2113568 | tf_op jit(solution)/shard_map/ppermute | solution.py:17
  85.9 3.5 %dynamic-slice_add_fusion = bf16[258,4096]{1,0:T(8,128)(2,1)S(1)} fusion(bf16[258,4096]{1,0:T(8,128)(2,1)} %collective-permute-done, bf16[258,12288]{1,0:T(8,128)(2,1)} %copy-done, s32[]{:T(128)S(6)} %select_n.19), kind=kLoop, calls=%fused_computation.30 | loop fusion | flops 4227072 | bytes 6340612 | tf_op jit(solution)/shard_map/add | solution.py:72
  89.5 1.9 %collective-permute-start.1 = (bf16[258,1024]{1,0:T(8,128)(2,1)S(1)}, bf16[258,1024]{1,0:T(8,128)(2,1)S(1)}, u32[]{:S(2)}, u32[]{:S(2)}) collective-permute-start(bf16[258,1024]{1,0:T(8,128)(2,1)S(1)} %slice.41), channel_id=1, source_target_pairs={{0,1},{1,2},{2,3},{3,4},{4,5},{5,6},{6,7},{7,8},{8,9},{9,10},{10,1... | collective-permute-start | bytes 1585160 | tf_op jit(solution)/shard_map/ppermute | solution.py:17
  91.4 10.5 %collective-permute-done.1 = bf16[258,1024]{1,0:T(8,128)(2,1)S(1)} collective-permute-done((bf16[258,1024]{1,0:T(8,128)(2,1)S(1)}, bf16[258,1024]{1,0:T(8,128)(2,1)S(1)}, u32[]{:S(2)}, u32[]{:S(2)}) %collective-permute-start.1) | collective-permute-done | bytes 528416 | tf_op jit(solution)/shard_map/ppermute | solution.py:17
  102.0 2.8 %multiply_convert_fusion.1 = (bf16[256,5120]{1,0:T(8,128)(2,1)}, bf16[256,5120]{1,0:T(8,128)(2,1)}) fusion(f32[5120]{0:T(1024)S(1)} %bitcast.27, bf16[258,4096]{1,0:T(8,128)(2,1)S(1)} %dynamic-slice_add_fusion, bf16[258,1024]{1,0:T(8,128)(2,1)S(1)} %collective-permute-done.1), kind=kLoop, calls=%fused_computation.26 | loop fusion | flops 9175040 | bytes 7905280 | tf_op jit(solution)/shard_map/convert_element_type | solution.py:28
  104.9 23.8 %concatenate.11 = bf16[515,5120]{1,0:T(8,128)(2,1)} concatenate(bf16[256,5120]{1,0:T(8,128)(2,1)} %get-tuple-element.63, bf16[256,5120]{1,0:T(8,128)(2,1)} %get-tuple-element.64, bf16[1,5120]{1,0:T(2,128)(2,1)S(1)} %pad_maximum_fusion, bf16[1,5120]{1,0:T(2,128)(2,1)S(1)} %get-tuple-element.62, bf16[1,5120]{1,0:T(2,128)(2,1)S(1)} %get-tuple-element.61), dimensions={0} | concatenate | bytes 10547200 | tf_op jit(solution)/shard_map/concatenate | solution.py:32
  128.7 38.6 %while.11 = (s32[]{:T(128)}, f32[8,256,512]{2,1,0:T(8,128)}, s32[8]{0:T(128)S(1)}, bf16[515,5120]{1,0:T(8,128)(2,1)}, s32[512]{0:T(512)S(1)}, /*index=5*/s32[512...) while((s32[]{:T(128)}, f32[8,256,512]{2,1,0:T(8,128)}, s32[8]{0:T(128)S(1)}, ...), condition=%wide.region_2.3_spmd.clone, body=%wide.region_1.2_spmd.clone.sunk | while | flops 813697024 | bytes 4248227 | solution.py:83
  128.7 0.6 dynamic_slice.24
  130.0 2.6 %fusion.32 = f32[515,512]{1,0:T(8,128)S(1)} fusion(bf16[515,5120]{1,0:T(8,128)(2,1)} %get-tuple-element.138, s32[]{:T(128)S(6)} %select_n.28, s32[512]{0:T(512)S(1)} %get-tuple-element.140, s32[512]{0:T(512)S(1)} %get-tuple-element.139), kind=kOutput, calls=%fused_computation.5.clone.1 | convolution fusion | flops 813170688 | bytes 2656260 | tf_op jit(solution)/shard_map/while/body/eval_jaxpr/dot_general | solution.py:81
  132.6 0.9 fusion.34
  133.6 0.6 dynamic_slice.24
  134.8 2.6 %fusion.32 = f32[515,512]{1,0:T(8,128)S(1)} fusion(bf16[515,5120]{1,0:T(8,128)(2,1)} %get-tuple-element.138, s32[]{:T(128)S(6)} %select_n.28, s32[512]{0:T(512)S(1)} %get-tuple-element.140, s32[512]{0:T(512)S(1)} %get-tuple-element.139), kind=kOutput, calls=%fused_computation.5.clone.1 | convolution fusion | flops 813170688 | bytes 2656260 | tf_op jit(solution)/shard_map/while/body/eval_jaxpr/dot_general | solution.py:81
  137.5 0.9 fusion.34
  138.4 0.6 dynamic_slice.24
  139.6 2.6 %fusion.32 = f32[515,512]{1,0:T(8,128)S(1)} fusion(bf16[515,5120]{1,0:T(8,128)(2,1)} %get-tuple-element.138, s32[]{:T(128)S(6)} %select_n.28, s32[512]{0:T(512)S(1)} %get-tuple-element.140, s32[512]{0:T(512)S(1)} %get-tuple-element.139), kind=kOutput, calls=%fused_computation.5.clone.1 | convolution fusion | flops 813170688 | bytes 2656260 | tf_op jit(solution)/shard_map/while/body/eval_jaxpr/dot_general | solution.py:81
  142.2 0.9 fusion.34
  143.2 0.6 dynamic_slice.24
  144.4 2.6 %fusion.32 = f32[515,512]{1,0:T(8,128)S(1)} fusion(bf16[515,5120]{1,0:T(8,128)(2,1)} %get-tuple-element.138, s32[]{:T(128)S(6)} %select_n.28, s32[512]{0:T(512)S(1)} %get-tuple-element.140, s32[512]{0:T(512)S(1)} %get-tuple-element.139), kind=kOutput, calls=%fused_computation.5.clone.1 | convolution fusion | flops 813170688 | bytes 2656260 | tf_op jit(solution)/shard_map/while/body/eval_jaxpr/dot_general | solution.py:81
  147.1 0.9 fusion.34
  148.0 0.6 dynamic_slice.24
  149.2 2.6 %fusion.32 = f32[515,512]{1,0:T(8,128)S(1)} fusion(bf16[515,5120]{1,0:T(8,128)(2,1)} %get-tuple-element.138, s32[]{:T(128)S(6)} %select_n.28, s32[512]{0:T(512)S(1)} %get-tuple-element.140, s32[512]{0:T(512)S(1)} %get-tuple-element.139), kind=kOutput, calls=%fused_computation.5.clone.1 | convolution fusion | flops 813170688 | bytes 2656260 | tf_op jit(solution)/shard_map/while/body/eval_jaxpr/dot_general | solution.py:81
  151.9 0.9 fusion.34
  152.8 0.6 dynamic_slice.24
  154.0 2.6 %fusion.32 = f32[515,512]{1,0:T(8,128)S(1)} fusion(bf16[515,5120]{1,0:T(8,128)(2,1)} %get-tuple-element.138, s32[]{:T(128)S(6)} %select_n.28, s32[512]{0:T(512)S(1)} %get-tuple-element.140, s32[512]{0:T(512)S(1)} %get-tuple-element.139), kind=kOutput, calls=%fused_computation.5.clone.1 | convolution fusion | flops 813170688 | bytes 2656260 | tf_op jit(solution)/shard_map/while/body/eval_jaxpr/dot_general | solution.py:81
  156.7 1.0 fusion.34
  157.6 0.6 dynamic_slice.24
  158.9 2.6 %fusion.32 = f32[515,512]{1,0:T(8,128)S(1)} fusion(bf16[515,5120]{1,0:T(8,128)(2,1)} %get-tuple-element.138, s32[]{:T(128)S(6)} %select_n.28, s32[512]{0:T(512)S(1)} %get-tuple-element.140, s32[512]{0:T(512)S(1)} %get-tuple-element.139), kind=kOutput, calls=%fused_computation.5.clone.1 | convolution fusion | flops 813170688 | bytes 2656260 | tf_op jit(solution)/shard_map/while/body/eval_jaxpr/dot_general | solution.py:81
  161.5 1.0 fusion.34
  162.5 0.6 dynamic_slice.24
  163.7 2.6 %fusion.32 = f32[515,512]{1,0:T(8,128)S(1)} fusion(bf16[515,5120]{1,0:T(8,128)(2,1)} %get-tuple-element.138, s32[]{:T(128)S(6)} %select_n.28, s32[512]{0:T(512)S(1)} %get-tuple-element.140, s32[512]{0:T(512)S(1)} %get-tuple-element.139), kind=kOutput, calls=%fused_computation.5.clone.1 | convolution fusion | flops 813170688 | bytes 2656260 | tf_op jit(solution)/shard_map/while/body/eval_jaxpr/dot_general | solution.py:81
  166.4 1.0 fusion.34
  167.3 4.8 %copy.6 = f32[8,32,8,512]{3,2,0,1:T(8,128)} copy(f32[8,32,8,512]{3,2,1,0:T(8,128)} %bitcast.8) | data formatting | bytes 8388608 | tf_op jit(solution)/shard_map/reshape | solution.py:84
  (19 shorter events, 0.3 us)
Async XLA Ops:
  52.4 2.7 %copy-start = (bf16[258,12288]{1,0:T(8,128)(2,1)}, bf16[258,12288]{1,0:T(8,128)(2,1)S(1)}, u32[]{:S(2)}) copy-start(bf16[258,12288]{1,0:T(8,128)(2,1)S(1)} %fusion.20) | copy-start | bytes 19021828
  56.0 30.0 %collective-permute-start = (bf16[258,4096]{1,0:T(8,128)(2,1)S(1)}, bf16[258,4096]{1,0:T(8,128)(2,1)}, u32[]{:S(2)}, u32[]{:S(2)}) collective-permute-start(bf16[258,4096]{1,0:T(8,128)(2,1)S(1)} %constant_dynamic-slice_fusion), channel_id=1, source_target_pairs={{0,1},{1,2},{2,3},{3,4},{4,5},{5,6},{6,7},{7,8},{8,9},{9,10},{10,1... | collective-permute-start | bytes 6340616 | tf_op jit(solution)/shard_map/ppermute | solution.py:17
  89.5 12.5 %collective-permute-start.1 = (bf16[258,1024]{1,0:T(8,128)(2,1)S(1)}, bf16[258,1024]{1,0:T(8,128)(2,1)S(1)}, u32[]{:S(2)}, u32[]{:S(2)}) collective-permute-start(bf16[258,1024]{1,0:T(8,128)(2,1)S(1)} %slice.41), channel_id=1, source_target_pairs={{0,1},{1,2},{2,3},{3,4},{4,5},{5,6},{6,7},{7,8},{8,9},{9,10},{10,1... | collective-permute-start | bytes 1585160 | tf_op jit(solution)/shard_map/ppermute | solution.py:17
where the time goes:
time: 173 us; the launch traced here: 172 us
  blocking collectives  40.4 us (23%)
  waiting for transfers between devices  38.5 us (22%)
  local copies, waits for them, and re-layouts  37.1 us (21%)
  other arithmetic  24.5 us (14%)
  matrix products  21 us (12%)
  loops' own time  5.37 us (3%)
  starting transfers between devices  3.84 us (2%)
    unnamed x1, blocking collectives  40.4 us
    ppermute x2, waiting for transfers between devices, shifted(): lax.ppermute(value, axis, [(source, source + steps) for source in range(i...  38.5 us
    concatenate x1, local copies, waits for them, and re-layouts, stacked(): jnp.concatenate([cross_terms, y_values, w_values[None, :], x_values[None,...  23.8 us
    dot_general x8, matrix products, one_block(): jnp.dot(window_piece, band_ones, preferred_element_type=jnp.float32)  21 us
    dynamic_update_slice x8, other arithmetic, per_device(): blocks = lax.map(one_block, jnp.arange(quota // BLOCK, dtype=jnp.int32))  7.51 us
    another operation x1, loops' own time, per_device(): blocks = lax.map(one_block, jnp.arange(quota // BLOCK, dtype=jnp.int32))  5.37 us
    convert_element_type x1, other arithmetic, per_device(): (returns.astype(jnp.float32) * weight[None, :]).astype(jnp.bfloat16)  5.16 us
    reshape x1, local copies, waits for them, and re-layouts, per_device(): return jnp.transpose(blocks, (1, 0, 2)).reshape(stocks, quota)  4.84 us
  transfers between devices with their start and end apart: 2, of which 2 were waited for; matrix products, arithmetic and copies ran while one was open for 0% of the time, Pallas kernels for 0%

commit v1 on v0

v1 whole, which is shorter than its diff:
```python
import functools

import jax
import jax.numpy as jnp
from jax import lax
from jax.experimental import pallas as pl
from jax.experimental.pallas import tpu as pltpu
from jax.sharding import PartitionSpec as P

WIN = 1024
RIDGE = 0.1
LANE = 128
STEP = 256
EXTRA = 16
TAIL = WIN // LANE + 1
MESH = pl.DeviceIdType.MESH


def pack_kernel(body, tiles_ref, own_ref, xw_ref, out_ref, sems):
    stocks = own_ref.shape[0]
    tiles = tiles_ref[0]
    before_tail = jnp.maximum(tiles - TAIL, 0)

    def copies(i):
        j = jnp.where(i < body, before_tail, tiles - TAIL) - body + i
        source = pl.ds(pl.multiple_of(jnp.maximum(j, 0) * LANE, LANE), LANE)
        target = pl.ds(pl.multiple_of(i * LANE, LANE), LANE)
        return (
            pltpu.make_async_copy(own_ref.at[:, source], out_ref.at[pl.ds(0, stocks), target], sems.at[0, i]),
            pltpu.make_async_copy(xw_ref.at[:, source], out_ref.at[pl.ds(stocks, EXTRA), target], sems.at[1, i]),
        )

    def begin(i, _):
        for copy in copies(i):
            copy.start()
        return 0

    def end(i, _):
        for copy in copies(i):
            copy.wait()
        return 0

    lax.fori_loop(0, body + TAIL, begin, 0)
    lax.fori_loop(0, body + TAIL, end, 0)


def exchange_kernel(n, body, packed_ref, spare_ref, count_ref, got_ref, counts_ref,
                    prev_buf, mine_buf, body_buf, small_send, small_recv,
                    sems_send, sems_recv, local_sems):
    me = lax.axis_index("span")
    right = lax.rem(me + 1, n)
    barrier = pltpu.get_barrier_semaphore()

    def greet(k, _):
        pl.semaphore_signal(barrier, inc=1, device_id=(lax.rem(me + k, n),), device_id_type=MESH)
        return 0

    lax.fori_loop(1, n, greet, 0)
    cut = TAIL * LANE
    mine = pltpu.make_async_copy(packed_ref.at[:, pl.ds(0, cut)], mine_buf, local_sems.at[0])
    mine.start()
    counts_ref[me] = count_ref[...]
    pl.semaphore_wait(barrier, n - 1)

    def part(index, first, width):
        return pltpu.make_async_remote_copy(
            src_ref=packed_ref.at[:, pl.ds(first, width)], dst_ref=got_ref.at[:, pl.ds(first, width)],
            send_sem=sems_send.at[index], recv_sem=sems_recv.at[index],
            device_id=(right,), device_id_type=MESH)

    tail_copy = part(0, body * LANE, cut)
    tail_copy.start()
    late_copy = part(1, cut, body * LANE - cut)
    late_copy.start()

    def small(k):
        return pltpu.make_async_remote_copy(
            src_ref=count_ref, dst_ref=counts_ref.at[me],
            send_sem=small_send.at[k], recv_sem=small_recv.at[k],
            device_id=(lax.rem(me + k, n),), device_id_type=MESH)

    def send_small(k, _):
        small(k).start()
        return 0

    lax.fori_loop(1, n, send_small, 0)
    mine.wait()
    tail_copy.wait_recv()
    fetch = pltpu.make_async_copy(got_ref.at[:, pl.ds(body * LANE, cut)], prev_buf, local_sems.at[1])
    fetch.start()
    fetch.wait()

    for i in range(TAIL):
        here = slice(i * LANE, (i + 1) * LANE)
        e = (TAIL - 1 - i) * LANE
        spare = spare_ref[0:1, here]
        body_buf[:, here] = mine_buf[:, here] * (1 - spare) + prev_buf[:, e:e + LANE] * spare

    body_copy = pltpu.make_async_remote_copy(
        src_ref=body_buf, dst_ref=got_ref.at[:, pl.ds(0, cut)],
        send_sem=sems_send.at[2], recv_sem=sems_recv.at[2],
        device_id=(right,), device_id_type=MESH)
    body_copy.start()

    def wait_small(k, _):
        small(k).wait()
        return 0

    lax.fori_loop(1, n, wait_small, 0)
    tail_copy.wait_send()
    late_copy.wait()
    body_copy.wait()


def regress_kernel(quota, body, own_ref, xw_ref, got_ref, counts_ref, me_ref, out_ref,
                   align_y, align_xw, tri, sums, carry):
    t = pl.program_id(0)
    lag = WIN // STEP
    me = me_ref[0]
    stocks = own_ref.shape[0]
    f32 = jnp.float32
    held = counts_ref[...].astype(f32)
    device = lax.broadcasted_iota(jnp.int32, held.shape, 0)

    def pick(condition):
        return jnp.max(jnp.sum(jnp.where(condition, held, 0.0), 0, keepdims=True)).astype(jnp.int32)

    own_count = pick(device == me)
    count_1 = pick(device == me - 1)
    count_2 = pick(device == me - 2)
    start = pick(device < me) - me * quota + WIN
    start_1 = start - count_1
    start_2 = start_1 - count_2
    tiles_1 = (count_1 + LANE - 1) // LANE
    tiles_2 = (count_2 + LANE - 1) // LANE
    gone = jnp.maximum(tiles_1 - TAIL, 0)

    @pl.when(t == 0)
    def _():
        k = lax.broadcasted_iota(jnp.int32, tri.shape, 0)
        col = lax.broadcasted_iota(jnp.int32, tri.shape, 1)
        tri[...] = jnp.where(k <= col, 1.0, 0.0).astype(jnp.bfloat16)
        carry[...] = jnp.zeros_like(carry)

    align_y[...] = jnp.zeros_like(align_y)
    align_xw[...] = jnp.zeros_like(align_xw)
    first = t * STEP
    width = STEP + LANE

    def add_piece(offset, low, high, columns, load):
        low_here = jnp.maximum(low, first - offset)
        high_here = jnp.minimum(high, first - offset + STEP)

        @pl.when(low_here < high_here)
        def _():
            tile = jnp.clip((first - offset + columns) // LANE - columns // LANE, 0, (columns - width) // LANE)
            at = pl.multiple_of(tile * LANE, LANE)
            c = lax.broadcasted_iota(jnp.int32, (width, STEP), 0) + at
            p = lax.broadcasted_iota(jnp.int32, (width, STEP), 1) + (first - offset)
            chosen = (c == p) & (c >= low) & (c < high)
            hot = jnp.where(chosen, 1.0, 0.0).astype(jnp.bfloat16)
            y, xw = load(pl.ds(at, width))
            align_y[...] += jnp.dot(y, hot, preferred_element_type=f32)
            align_xw[...] += jnp.dot(xw, hot, preferred_element_type=f32)

    def load_own(s):
        return own_ref[:, s], xw_ref[:, s]

    def load_got(s):
        return got_ref[pl.ds(0, stocks), s], got_ref[pl.ds(stocks, EXTRA), s]

    capacity = own_ref.shape[1]
    add_piece(start, 0, own_count, capacity, load_own)
    base = (body + TAIL - tiles_1) * LANE
    add_piece(start_1 - base, jnp.maximum(base, 0), base + count_1, got_ref.shape[1], load_got)
    free = jnp.minimum(body - gone, TAIL) * LANE

    @pl.when((t < lag) & (start_1 > first))
    def _():
        c = lax.broadcasted_iota(jnp.int32, (TAIL * LANE, STEP), 0)
        p = lax.broadcasted_iota(jnp.int32, (TAIL * LANE, STEP), 1) + (first - start_2)
        slot = c // LANE
        source = (tiles_2 - 1 - 2 * slot) * LANE + c
        chosen = (source == p) & (c < free) & (source >= 0) & (source < count_2)
        hot = jnp.where(chosen, 1.0, 0.0).astype(jnp.bfloat16)
        y, xw = load_got(pl.ds(0, TAIL * LANE))
        align_y[...] += jnp.dot(y, hot, preferred_element_type=f32)
        align_xw[...] += jnp.dot(xw, hot, preferred_element_type=f32)

    w = align_xw[1:2, :]
    x = align_xw[0:1, :] * w
    y = align_y[...] * w
    cross = (x * y).astype(jnp.bfloat16)
    square = (x * x).astype(jnp.bfloat16)
    row = lax.broadcasted_iota(jnp.int32, (EXTRA, STEP), 0)
    small = jnp.where(row == 0, w, jnp.where(row == 1, x, jnp.where(row == 2, square.astype(f32), 0.0)))
    slot = lax.rem(t, lag + 1)
    old = lax.rem(t + 1, lag + 1)

    def window(lo, size, value):
        rows = pl.ds(lo, size)
        now = jnp.dot(value.astype(jnp.bfloat16), tri[...], preferred_element_type=f32)
        before = jnp.where(t >= lag, sums[old, rows, :], 0.0)
        result = carry[rows, :] + (now - before)
        sums[slot, rows, :] = now
        carry[rows, :] = jnp.broadcast_to(result[:, STEP - 1:], (size, STEP))
        return result

    sum_small = window(2 * stocks, EXTRA, small)
    sum_w = sum_small[0:1]
    sum_x = sum_small[1:2]
    sum_xx = sum_small[2:3]
    sum_xy = window(0, stocks, cross)
    sum_y = window(stocks, stocks, y)
    numerator = sum_w * sum_xy - sum_x * sum_y
    denominator = sum_w * sum_xx - sum_x * sum_x + RIDGE * WIN * WIN
    out_ref[...] = numerator / denominator


def per_device(n, returns, market, mask, counts):
    stocks, capacity = returns.shape
    quota = capacity // 2
    body = quota // LANE + 1
    bf16 = jnp.bfloat16
    columns = (body + TAIL) * LANE
    rows = stocks + EXTRA
    xw = jnp.concatenate([market[None, :], mask.astype(bf16)[None, :],
                          jnp.zeros((EXTRA - 2, capacity), bf16)], 0)
    count_tile = jnp.broadcast_to(counts[:, None], (8, LANE))
    tiles = (counts + (LANE - 1)) // LANE
    slots = jnp.arange(TAIL * LANE, dtype=jnp.int32) // LANE
    free = (jnp.maximum(tiles - TAIL, 0) - body + slots < 0).astype(bf16)
    vmem = pl.BlockSpec(memory_space=pltpu.VMEM)
    hbm = pl.BlockSpec(memory_space=pltpu.HBM)
    packed = pl.pallas_call(
        functools.partial(pack_kernel, body),
        out_shape=jax.ShapeDtypeStruct((rows, columns), bf16),
        in_specs=[pl.BlockSpec(memory_space=pltpu.SMEM), hbm, hbm],
        out_specs=vmem,
        scratch_shapes=[pltpu.SemaphoreType.DMA((2, body + TAIL))],
        compiler_params=pltpu.CompilerParams(vmem_limit_bytes=16 * 2**20),
        name="pack",
    )(tiles, returns, xw)
    tail_shape = (rows, TAIL * LANE)
    got, gathered = pl.pallas_call(
        functools.partial(exchange_kernel, n, body),
        out_shape=(jax.ShapeDtypeStruct((rows, columns), bf16),
                   jax.ShapeDtypeStruct((n, 8, LANE), jnp.int32)),
        in_specs=[hbm, vmem, vmem],
        out_specs=(hbm, vmem),
        scratch_shapes=[
            pltpu.VMEM(tail_shape, bf16),
            pltpu.VMEM(tail_shape, bf16),
            pltpu.VMEM(tail_shape, bf16),
            pltpu.SemaphoreType.DMA((n,)),
            pltpu.SemaphoreType.DMA((n,)),
            pltpu.SemaphoreType.DMA((3,)),
            pltpu.SemaphoreType.DMA((3,)),
            pltpu.SemaphoreType.DMA((2,)),
        ],
        compiler_params=pltpu.CompilerParams(
            collective_id=0, has_side_effects=True, vmem_limit_bytes=16 * 2**20),
        name="exchange",
    )(packed, jnp.broadcast_to(free[None, :], (EXTRA, TAIL * LANE)), count_tile)
    me = lax.axis_index("span").astype(jnp.int32).reshape(1)
    steps = (quota + WIN) // STEP
    lag = WIN // STEP

    def whole(*shape):
        return pl.BlockSpec(shape, lambda t, me: (0,) * len(shape))

    return pl.pallas_call(
        lambda m, a, b, c, d, *rest: regress_kernel(quota, body, a, b, c, d, m, *rest),
        out_shape=jax.ShapeDtypeStruct((stocks, quota), jnp.float32),
        grid_spec=pltpu.PrefetchScalarGridSpec(
            num_scalar_prefetch=1,
            grid=(steps,),
            in_specs=[whole(stocks, capacity), whole(EXTRA, capacity), whole(rows, columns), whole(n, LANE)],
            out_specs=pl.BlockSpec((stocks, STEP), lambda t, me: (0, jnp.maximum(t - lag, 0))),
            scratch_shapes=[
                pltpu.VMEM((stocks, STEP), jnp.float32),
                pltpu.VMEM((EXTRA, STEP), jnp.float32),
                pltpu.VMEM((STEP, STEP), bf16),
                pltpu.VMEM((lag + 1, 2 * stocks + EXTRA, STEP), jnp.float32),
                pltpu.VMEM((2 * stocks + EXTRA, STEP), jnp.float32),
            ],
        ),
        compiler_params=pltpu.CompilerParams(vmem_limit_bytes=56 * 2**20),
        name="regress",
    )(me, returns, xw, got, gathered[:, 0, :])


def solution(mesh):
    return jax.shard_map(
        functools.partial(per_device, mesh.shape["span"]),
        mesh=mesh,
        in_specs=(P(None, "span"), P("span"), P("span"), P("span")),
        out_specs=P(None, "span"),
        check_vma=False,
    )
```

time: 173 us -> 74.6 us (0.43)
  the two profiles are of different devices: /device:TPU:8 before, /device:TPU:0 now
where the time goes in v1:
time: 74.6 us; the launch traced here: 74.3 us
  Pallas kernels  67.4 us (90%)
  local copies, waits for them, and re-layouts  5.24 us (7%)
  other arithmetic  0.89 us (1%)
  between operations  0.75 us (1%)
    pallas_call x1, Pallas kernels, per_device(): pl.pallas_call(functools.partial(exchange_kernel, n, body), out_shape=(ja...  42.6 us
    pallas_call x1, Pallas kernels, per_device(): pl.pallas_call(lambda m, a, b, c, d, *rest: regress_kernel(quota, body, a...  22.4 us
    unnamed x6, local copies, waits for them, and re-layouts  3.77 us
    pallas_call x1, Pallas kernels, per_device(): pl.pallas_call(functools.partial(pack_kernel, body), out_shape=jax.ShapeD...  2.39 us

profile of v1, /device:TPU:0, one launch (start us, length us, event | category | flops | bytes accessed | tf_op | source)
XLA Modules:
  0.0 74.3 jit_solution(14233939525410813184)
XLA Ops:
  0.7 0.1 pad.2.clone
  0.8 0.8 %convert_element_type.10 = bf16[8192]{0:T(1024)(128)(2,1)S(1)} convert(s32[8192]{0:T(1024)} %param.6) | non-fusion elementwise | flops 8192 | bytes 49152 | tf_op jit(solution)/shard_map/convert_element_type | solution.py:227
  1.6 0.7 broadcast_in_dim.23
  2.3 0.1 maximum_maximum_fusion.xw_ref.b
  2.4 0.0 copy-start
  2.5 2.2 %copy-done = bf16[256,8192]{1,0:T(8,128)(2,1)S(1)} copy-done((bf16[256,8192]{1,0:T(8,128)(2,1)S(1)}, bf16[256,8192]{1,0:T(8,128)(2,1)}, u32[]{:S(2)}) %copy-start) | copy-done | bytes 4194328
  4.6 0.0 copy-start.2
  4.6 2.4 %pack.1.packed_ref = bf16[272,5376]{1,0:T(8,128)(2,1)S(1)} custom-call(s32[1]{0:T(128)S(6)} %select_n.14.tiles_ref, bf16[256,8192]{1,0:T(8,128)(2,1)S(1)} %copy-done, bf16[16,8192]{1,0:T(8,128)(2,1)S(1)} %maximum_maximum_fusion.xw_ref.b), custom_call_target="tpu_custom_call" | custom-call | tf_op jit(solution)/shard_map/pack/pallas_call | solution.py:235
  7.0 42.6 %exchange.1 = (bf16[272,5376]{1,0:T(8,128)(2,1)S(1)}, s32[32,8,128]{2,1,0:T(8,128)S(1)}) custom-call(bf16[272,5376]{1,0:T(8,128)(2,1)S(1)} %pack.1.packed_ref, bf16[16,1152]{1,0:T(8,128)(2,1)S(1)} %broadcast_in_dim.26.spare_ref, s32[8,128]{1,0:T(8,128)S(1)} %broadcast_in_dim.28.count_ref), custom_call_target="tpu_custom_call" | custom-call | tf_op jit(solution)/shard_map/exchange/pallas_call | solution.py:245
  49.7 0.0 copy-done.2
  49.7 0.0 copy-start.1
  49.7 1.6 %copy-done.1 = bf16[272,5376]{1,0:T(8,128)(2,1)} copy-done((bf16[272,5376]{1,0:T(8,128)(2,1)}, bf16[272,5376]{1,0:T(8,128)(2,1)S(1)}, u32[]{:S(2)}) %copy-start.1) | copy-done | bytes 2924568
  51.3 0.6 slice_bitcast_fusion.d
  51.9 22.4 %regress.1 = f32[256,4096]{1,0:T(8,128)} custom-call(s32[1]{0:T(128)} %bitcast.m, bf16[256,8192]{1,0:T(8,128)(2,1)} %a.1, bf16[16,8192]{1,0:T(8,128)(2,1)} %copy-done.2, bf16[272,5376]{1,0:T(8,128)(2,1)} %copy-done.1, s32[32,128]{1,0:T(8,128)} %slice_bitcast_fusion.d), custom_call_target="tpu_custom_call" | custom-call | tf_op jit(solution)/shard_map/regress/pallas_call | solution.py:272
  (6 shorter events, 0.1 us)
Async XLA Ops:
  2.4 2.2 %copy-start = (bf16[256,8192]{1,0:T(8,128)(2,1)S(1)}, bf16[256,8192]{1,0:T(8,128)(2,1)}, u32[]{:S(2)}) copy-start(bf16[256,8192]{1,0:T(8,128)(2,1)} %a.1) | copy-start | bytes 12582916
  4.6 45.0 %copy-start.2 = (bf16[16,8192]{1,0:T(8,128)(2,1)}, bf16[16,8192]{1,0:T(8,128)(2,1)S(1)}, u32[]{:S(2)}) copy-start(bf16[16,8192]{1,0:T(8,128)(2,1)S(1)} %maximum_maximum_fusion.xw_ref.b) | copy-start | bytes 786436
  49.7 1.6 %copy-start.1 = (bf16[272,5376]{1,0:T(8,128)(2,1)}, bf16[272,5376]{1,0:T(8,128)(2,1)S(1)}, u32[]{:S(2)}) copy-start(bf16[272,5376]{1,0:T(8,128)(2,1)S(1)} %get-tuple-element.7.c) | copy-start | bytes 8773636

commit v2 on v0

v2 whole, which is shorter than its diff:
```python
import functools

import jax
import jax.numpy as jnp
from jax import lax
from jax.experimental import pallas as pl
from jax.experimental.pallas import tpu as pltpu
from jax.sharding import PartitionSpec as P

WIN = 1024
RIDGE = 0.1
LANE = 128
STEP = 256
SUBS = 2
HALF = 8
TAIL = WIN // LANE + 1
MESH = pl.DeviceIdType.MESH


def pack_kernel(body, count_ref, own_ref, market_ref, mask_ref,
                packed_ref, own_xw_ref, packed_xw_ref, spare_ref, tile_ref):
    count = count_ref[0]
    tiles = (count + (LANE - 1)) // LANE
    before_tail = jnp.maximum(tiles - TAIL, 0)
    dense = market_ref.shape[0]
    half = packed_xw_ref.shape[0] // 2
    own_xw_ref[pl.ds(0, dense), :] = market_ref[...].astype(jnp.float32)
    own_xw_ref[pl.ds(dense, dense), :] = mask_ref[...].astype(jnp.float32)
    packed_xw_ref[...] = jnp.zeros_like(packed_xw_ref)
    tile_ref[...] = jnp.full(tile_ref.shape, count, jnp.int32)

    def fill(i, _):
        j = jnp.where(i < body, before_tail, tiles - TAIL) - body + i
        row = jnp.maximum(j, 0)
        source = pl.ds(pl.multiple_of(row * LANE, LANE), LANE)
        packed_ref[:, pl.ds(pl.multiple_of(i * LANE, LANE), LANE)] = own_ref[:, source]
        packed_xw_ref[pl.ds(i, 1), :] = own_xw_ref[pl.ds(row, 1), :]
        packed_xw_ref[pl.ds(half + i, 1), :] = own_xw_ref[pl.ds(dense + row, 1), :]
        return 0

    lax.fori_loop(0, body + TAIL, fill, 0)
    for i in range(TAIL):
        free = jnp.where(before_tail - body + i < 0, 1.0, 0.0)
        spare_ref[:, i * LANE:(i + 1) * LANE] = jnp.full((spare_ref.shape[0], LANE), free, jnp.float32)


def exchange_kernel(n, body, packed_ref, packed_xw_ref, spare_ref, count_ref,
                    got_ref, got_xw_ref, got_free_ref, counts_ref,
                    body_buf, free_buf, small_send, small_recv, sems_send, sems_recv):
    me = lax.axis_index("span")
    right = lax.rem(me + 1, n)
    barrier = pltpu.get_barrier_semaphore()

    def greet(k, _):
        pl.semaphore_signal(barrier, inc=1, device_id=(lax.rem(me + k, n),), device_id_type=MESH)
        return 0

    lax.fori_loop(1, n, greet, 0)
    cut = TAIL * LANE
    half = packed_xw_ref.shape[0] // 2
    half_free = free_buf.shape[0] // 2
    counts_ref[me] = count_ref[...]
    free_buf[...] = jnp.zeros_like(free_buf)
    pl.semaphore_wait(barrier, n - 1)

    def to_right(index, source, target):
        return pltpu.make_async_remote_copy(
            src_ref=source, dst_ref=target, send_sem=sems_send.at[index], recv_sem=sems_recv.at[index],
            device_id=(right,), device_id_type=MESH)

    def part(index, first, width):
        return to_right(index, packed_ref.at[:, pl.ds(first, width)], got_ref.at[:, pl.ds(first, width)])

    xw_copy = to_right(3, packed_xw_ref, got_xw_ref)
    xw_copy.start()
    tail_copy = part(0, body * LANE, cut)
    tail_copy.start()
    late_copy = part(1, cut, body * LANE - cut)
    late_copy.start()

    def small(k):
        return pltpu.make_async_remote_copy(
            src_ref=count_ref, dst_ref=counts_ref.at[me],
            send_sem=small_send.at[k], recv_sem=small_recv.at[k],
            device_id=(lax.rem(me + k, n),), device_id_type=MESH)

    def send_small(k, _):
        small(k).start()
        return 0

    lax.fori_loop(1, n, send_small, 0)
    xw_copy.wait_recv()
    tail_copy.wait_recv()

    for i in range(TAIL):
        here = slice(i * LANE, (i + 1) * LANE)
        row = body + TAIL - 1 - i
        free = spare_ref[0:1, here]
        spare = free.astype(jnp.bfloat16)
        body_buf[:, here] = packed_ref[:, here] * (1 - spare) + got_ref[:, row * LANE:(row + 1) * LANE] * spare
        free_buf[i:i + 1, :] = got_xw_ref[row:row + 1, :]
        free_buf[half_free + i:half_free + i + 1, :] = got_xw_ref[half + row:half + row + 1, :]

    body_copy = to_right(2, body_buf, got_ref.at[:, pl.ds(0, cut)])
    body_copy.start()
    free_copy = to_right(4, free_buf, got_free_ref)
    free_copy.start()

    def wait_small(k, _):
        small(k).wait()
        return 0

    lax.fori_loop(1, n, wait_small, 0)
    xw_copy.wait_send()
    tail_copy.wait_send()
    late_copy.wait()
    body_copy.wait()
    free_copy.wait()


def regress_kernel(quota, body, own_ref, own_xw_ref, got_ref, got_xw_ref, free_ref, counts_ref, out_ref,
                   facts, hot_own, hot_got, pair, align, history, small_history, carry):
    t = pl.program_id(0)
    me = lax.axis_index("span")
    stocks, capacity = own_ref.shape
    columns = got_ref.shape[1]
    f32, bf16 = jnp.float32, jnp.bfloat16
    width = STEP + LANE

    def hot_of(low, high, shift, rows):
        c = lax.broadcasted_iota(jnp.int32, (rows, STEP), 0)
        p = lax.broadcasted_iota(jnp.int32, (rows, STEP), 1)
        return jnp.where((c == p + shift) & (c >= low) & (c < high), 1.0, 0.0).astype(bf16)

    @pl.when(t == 0)
    def _():
        held = counts_ref[:, 0, :].astype(f32)
        device = lax.broadcasted_iota(jnp.int32, held.shape, 0)

        def pick(condition):
            return jnp.max(jnp.sum(jnp.where(condition, held, 0.0), 0, keepdims=True)).astype(jnp.int32)

        own_count = pick(device == me)
        count_1 = pick(device == me - 1)
        count_2 = pick(device == me - 2)
        start = pick(device < me) - me * quota + WIN
        facts[0] = own_count
        facts[1] = count_1
        facts[2] = count_2
        facts[3] = start
        base = (body + TAIL - (count_1 + LANE - 1) // LANE) * LANE
        hot_own[...] = hot_of(0, width, lax.rem(columns + LANE * LANE - start, LANE), width)
        hot_got[...] = hot_of(0, width, lax.rem(columns + LANE * LANE - (start - count_1 - base), LANE), width)
        k = lax.broadcasted_iota(jnp.int32, (STEP, STEP), 0)
        col = lax.broadcasted_iota(jnp.int32, (STEP, STEP), 1)
        pair[pl.ds(0, STEP), :] = jnp.where(k <= col, 1.0, 0.0).astype(bf16)
        pair[pl.ds(STEP, STEP), :] = jnp.where(k <= col, -1.0, 0.0).astype(bf16)
        carry[...] = jnp.zeros_like(carry)
        history[:, pl.ds(0, WIN)] = jnp.zeros((2 * stocks, WIN), bf16)
        small_history[:, pl.ds(0, WIN)] = jnp.zeros((HALF, WIN), f32)

    own_count = facts[0]
    count_1 = facts[1]
    count_2 = facts[2]
    start = facts[3]
    start_1 = start - count_1
    start_2 = start_1 - count_2
    tiles_1 = (count_1 + LANE - 1) // LANE
    tiles_2 = (count_2 + LANE - 1) // LANE
    base = (body + TAIL - tiles_1) * LANE
    free = jnp.minimum(body - jnp.maximum(tiles_1 - TAIL, 0), TAIL) * LANE
    dense = own_xw_ref.shape[0] // 2
    half = got_xw_ref.shape[0] // 2
    half_free = free_ref.shape[0] // 2

    def wide(ref, first_row, count):
        return jnp.concatenate([ref[pl.ds(first_row + i, 1), :] for i in range(count)], 1)

    def lift(y, x, w):
        row = lax.broadcasted_iota(jnp.int32, (16, x.shape[1]), 0)
        return jnp.concatenate([y, jnp.where(row == 0, x, w).astype(bf16)], 0)

    def load_own(tile):
        y = own_ref[:, pl.ds(pl.multiple_of(tile * LANE, LANE), width)]
        return lift(y, wide(own_xw_ref, tile, width // LANE), wide(own_xw_ref, dense + tile, width // LANE))

    def load_got(tile):
        y = got_ref[:, pl.ds(pl.multiple_of(tile * LANE, LANE), width)]
        return lift(y, wide(got_xw_ref, tile, width // LANE), wide(got_xw_ref, half + tile, width // LANE))

    def dot(a, b):
        return jnp.dot(a, b, preferred_element_type=f32)

    def gather(s):
        first = t * (SUBS * STEP) + s * STEP

        def plan(offset, low, high, total):
            head = first - offset
            floor = (head + columns) // LANE - columns // LANE
            tile = jnp.clip(floor, 0, (total - width) // LANE)
            inside = (low <= head) & (head + STEP <= high) & (tile == floor)
            touched = jnp.maximum(low, head) < jnp.minimum(high, head + STEP)
            at = tile * LANE
            return inside, touched, tile, (low - at, high - at, head - at)

        own_in, own_any, own_tile, own_map = plan(start, 0, own_count, capacity)
        got_in, got_any, got_tile, got_map = plan(
            start_1 - base, jnp.maximum(base, 0), base + count_1, columns)

        @pl.when(own_in)
        def _():
            align[s] = dot(load_own(own_tile), hot_own[...])

        @pl.when(got_in)
        def _():
            align[s] = dot(load_got(got_tile), hot_got[...])

        @pl.when(jnp.logical_not(own_in | got_in))
        def _():
            align[s] = jnp.zeros(align.shape[1:], f32)

            @pl.when(own_any)
            def _():
                align[s] += dot(load_own(own_tile), hot_of(*own_map, width))

            @pl.when(got_any)
            def _():
                align[s] += dot(load_got(got_tile), hot_of(*got_map, width))

            @pl.when((first < WIN) & (start_1 > first))
            def _():
                c = lax.broadcasted_iota(jnp.int32, (TAIL * LANE, STEP), 0)
                p = lax.broadcasted_iota(jnp.int32, (TAIL * LANE, STEP), 1) + (first - start_2)
                source = (tiles_2 - 1 - 2 * (c // LANE)) * LANE + c
                chosen = (source == p) & (c < free) & (source >= 0) & (source < count_2)
                hot = jnp.where(chosen, 1.0, 0.0).astype(bf16)
                align[s] += dot(lift(got_ref[:, pl.ds(0, TAIL * LANE)], wide(free_ref, 0, TAIL),
                                     wide(free_ref, half_free, TAIL)), hot)

    for s in range(SUBS):
        gather(s)

    small_rows = lax.broadcasted_iota(jnp.int32, (HALF, STEP), 0)
    moments = []
    both = pair[...]
    for s in range(SUBS):
        q = pl.multiple_of(t * (SUBS * STEP) + s * STEP, STEP)
        now_at = pl.ds(q + WIN, STEP)
        old_at = pl.ds(q, STEP)
        w = align[s, stocks + 1:stocks + 2, :]
        x = align[s, stocks:stocks + 1, :] * w
        y = align[s, 0:stocks, :] * w
        cross = (x * y).astype(bf16)
        y = y.astype(bf16)
        square = (x * x).astype(bf16).astype(f32)
        small = jnp.where(small_rows == 0, w, jnp.where(small_rows == 1, x, square))
        parts = []
        history[pl.ds(0, stocks), now_at] = cross
        history[pl.ds(stocks, stocks), now_at] = y
        small_history[:, now_at] = small
        pieces = (
            (0, stocks, cross, history[pl.ds(0, stocks), old_at]),
            (stocks, stocks, y, history[pl.ds(stocks, stocks), old_at]),
            (2 * stocks, HALF, small.astype(bf16), small_history[:, old_at].astype(bf16)),
        )
        for lo, size, now, old in pieces:
            change = dot(jnp.concatenate([now, old], 1), both)
            rows = pl.ds(lo, size)
            held = carry[rows, :]
            result = change + jnp.concatenate([held] * (STEP // LANE), 1)
            carry[rows, :] = jnp.broadcast_to(result[:, STEP - 1:], (size, LANE))
            parts.append(result)
        sum_xy, sum_y, tiny = parts
        sum_w = tiny[0:1]
        sum_x = tiny[1:2]
        sum_xx = tiny[2:3]
        inverse = 1.0 / (sum_w * sum_xx - sum_x * sum_x + RIDGE * WIN * WIN)
        out_ref[:, s * STEP:(s + 1) * STEP] = (sum_w * inverse) * sum_xy - (sum_x * inverse) * sum_y


def per_device(n, returns, market, mask, counts):
    stocks, capacity = returns.shape
    quota = capacity // 2
    body = quota // LANE + 1
    bf16, f32, i32 = jnp.bfloat16, jnp.float32, jnp.int32
    slots = body + TAIL
    columns = slots * LANE
    dense = capacity // LANE
    half = -(-slots // 8) * 8
    half_free = -(-TAIL // 8) * 8
    shape = jax.ShapeDtypeStruct
    vmem = pl.BlockSpec(memory_space=pltpu.VMEM)
    packed, own_xw, packed_xw, spare, count_tile = pl.pallas_call(
        functools.partial(pack_kernel, body),
        out_shape=(shape((stocks, columns), bf16), shape((2 * dense, LANE), f32), shape((2 * half, LANE), f32),
                   shape((8, TAIL * LANE), f32), shape((8, LANE), i32)),
        in_specs=[pl.BlockSpec(memory_space=pltpu.SMEM), vmem, vmem, vmem],
        out_specs=(vmem,) * 5,
        compiler_params=pltpu.CompilerParams(vmem_limit_bytes=16 * 2**20),
        name="pack",
    )(counts, returns, market.reshape(dense, LANE), mask.reshape(dense, LANE))
    got, got_xw, got_free, gathered = pl.pallas_call(
        functools.partial(exchange_kernel, n, body),
        out_shape=(shape((stocks, columns), bf16), shape((2 * half, LANE), f32),
                   shape((2 * half_free, LANE), f32), shape((n, 8, LANE), i32)),
        in_specs=[vmem] * 4,
        out_specs=(vmem,) * 4,
        scratch_shapes=[
            pltpu.VMEM((stocks, TAIL * LANE), bf16),
            pltpu.VMEM((2 * half_free, LANE), f32),
            pltpu.SemaphoreType.DMA((n,)),
            pltpu.SemaphoreType.DMA((n,)),
            pltpu.SemaphoreType.DMA((5,)),
            pltpu.SemaphoreType.DMA((5,)),
        ],
        compiler_params=pltpu.CompilerParams(
            collective_id=0, has_side_effects=True, vmem_limit_bytes=16 * 2**20),
        name="exchange",
    )(packed, packed_xw, spare, count_tile)
    steps = (quota + WIN) // (SUBS * STEP)
    lag = WIN // (SUBS * STEP)
    return pl.pallas_call(
        functools.partial(regress_kernel, quota, body),
        out_shape=shape((stocks, quota), f32),
        grid=(steps,),
        in_specs=[vmem] * 6,
        out_specs=pl.BlockSpec((stocks, SUBS * STEP), lambda t: (0, jnp.maximum(t - lag, 0))),
        scratch_shapes=[
            pltpu.SMEM((4,), i32),
            pltpu.VMEM((STEP + LANE, STEP), bf16),
            pltpu.VMEM((STEP + LANE, STEP), bf16),
            pltpu.VMEM((2 * STEP, STEP), bf16),
            pltpu.VMEM((SUBS, stocks + 16, STEP), f32),
            pltpu.VMEM((2 * stocks, quota + 2 * WIN), bf16),
            pltpu.VMEM((HALF, quota + 2 * WIN), f32),
            pltpu.VMEM((2 * stocks + HALF, LANE), f32),
        ],
        compiler_params=pltpu.CompilerParams(vmem_limit_bytes=32 * 2**20),
        name="regress",
    )(returns, own_xw, got, got_xw, got_free, gathered)


def solution(mesh):
    return jax.shard_map(
        functools.partial(per_device, mesh.shape["span"]),
        mesh=mesh,
        in_specs=(P(None, "span"), P("span"), P("span"), P("span")),
        out_specs=P(None, "span"),
        check_vma=False,
    )
```

time: 173 us -> 62.1 us (0.36)
  the two profiles are of different devices: /device:TPU:8 before, /device:TPU:0 now
where the time goes in v2:
time: 62.1 us; the launch traced here: 61.8 us
  Pallas kernels  57.5 us (93%)
  local copies, waits for them, and re-layouts  3.66 us (6%)
  between operations  0.69 us (1%)
    pallas_call x1, Pallas kernels, per_device(): pl.pallas_call(functools.partial(exchange_kernel, n, body), out_shape=(sh...  41.5 us
    pallas_call x1, Pallas kernels, per_device(): pl.pallas_call(functools.partial(regress_kernel, quota, body), out_shape=...  15 us
    unnamed x8, local copies, waits for them, and re-layouts  3.66 us

profile of v2, /device:TPU:0, one launch (start us, length us, event | category | flops | bytes accessed | tf_op | source)
XLA Modules:
  0.0 61.8 jit_solution(7606359848738839710)
XLA Ops:
  0.7 0.0 copy-start
  0.7 2.2 %copy-done = bf16[256,8192]{1,0:T(8,128)(2,1)S(1)} copy-done((bf16[256,8192]{1,0:T(8,128)(2,1)S(1)}, bf16[256,8192]{1,0:T(8,128)(2,1)}, u32[]{:S(2)}) %copy-start) | copy-done | bytes 4194328
  2.8 0.0 copy-start.2
  2.8 0.8 %copy-done.2 = s32[8192]{0:T(1024)S(1)} copy-done((s32[8192]{0:T(1024)S(1)}, s32[8192]{0:T(1024)}, u32[]{:S(2)}) %copy-start.2) | copy-done | bytes 32792
  3.6 0.0 copy-start.3
  3.6 0.7 %copy-done.3 = bf16[8192]{0:T(1024)(128)(2,1)S(1)} copy-done((bf16[8192]{0:T(1024)(128)(2,1)S(1)}, bf16[8192]{0:T(1024)(128)(2,1)}, u32[]{:S(2)}) %copy-start.3) | copy-done | bytes 16408
  4.3 0.0 copy-start.1
  4.3 1.1 %pack.1 = (bf16[256,5376]{1,0:T(8,128)(2,1)S(1)}, f32[128,128]{1,0:T(8,128)S(1)}, f32[96,128]{1,0:T(8,128)S(1)}, f32[8,1152]{1,0:T(8,128)S(1)}, s32[8,128]{1,0:T(8,128)S(1)}) custom-call(s32[1]{0:T(128)S(6)} %copy.5.count_ref, bf16[256,8192]{1,0:T(8,128)(2,1)S(1)} %copy-done, bf16[64,128]{1,0:T(8,128)(2,1)S(1)} %bitcast.3, s32[64,128]{1,0:T(8,128)S(1)} %bitcast.2), custom_call_target="tpu_custom_call" | custom-call | tf_op jit(solution)/shard_map/pack/pallas_call | solution.py:293
  5.4 41.5 %exchange.1 = (bf16[256,5376]{1,0:T(8,128)(2,1)S(1)}, f32[96,128]{1,0:T(8,128)S(1)}, f32[32,128]{1,0:T(8,128)S(1)}, s32[32,8,128]{2,1,0:T(8,128)S(1)}) custom-call(bf16[256,5376]{1,0:T(8,128)(2,1)S(1)} %get-tuple-element.15.packed_ref, f32[96,128]{1,0:T(8,128)S(1)} %get-tuple-element.16.packed_xw_ref, f32[8,1152]{1,0:T(8,128)S(1)} %get-tuple-element.17.spare_ref, ...), custom_call_target="tpu_custom_call" | custom-call | tf_op jit(solution)/shard_map/exchange/pallas_call | solution.py:302
  46.9 0.0 copy-done.1
  46.9 15.0 %regress.1 = f32[256,4096]{1,0:T(8,128)} custom-call(bf16[256,8192]{1,0:T(8,128)(2,1)S(1)} %copy-done.1, f32[128,128]{1,0:T(8,128)S(1)} %get-tuple-element.14.own_xw_ref, bf16[256,5376]{1,0:T(8,128)(2,1)S(1)} %get-tuple-element.19.got_ref, f32[96,128]{1,0:T(8,128)S(1)} %get-tuple-element.20.got_xw_ref, f32[32,128]{1,0:T(8,128)S(1)} %get-tuple-element.21.free_ref, ...), custom_call_target="tpu_custom_call" | custom-call | tf_op jit(solution)/shard_map/regress/pallas_call | solution.py:322
Async XLA Ops:
  0.7 2.2 %copy-start = (bf16[256,8192]{1,0:T(8,128)(2,1)S(1)}, bf16[256,8192]{1,0:T(8,128)(2,1)}, u32[]{:S(2)}) copy-start(bf16[256,8192]{1,0:T(8,128)(2,1)} %own_ref.3) | copy-start | bytes 12582916
  2.8 0.8 %copy-start.2 = (s32[8192]{0:T(1024)S(1)}, s32[8192]{0:T(1024)}, u32[]{:S(2)}) copy-start(s32[8192]{0:T(1024)} %param.6) | copy-start | bytes 98308
  3.6 0.7 %copy-start.3 = (bf16[8192]{0:T(1024)(128)(2,1)S(1)}, bf16[8192]{0:T(1024)(128)(2,1)}, u32[]{:S(2)}) copy-start(bf16[8192]{0:T(1024)(128)(2,1)} %param.5) | copy-start | bytes 49156
  4.3 42.6 %copy-start.1 = (bf16[256,8192]{1,0:T(8,128)(2,1)S(1)}, bf16[256,8192]{1,0:T(8,128)(2,1)}, u32[]{:S(2)}) copy-start(bf16[256,8192]{1,0:T(8,128)(2,1)} %own_ref.3) | copy-start | bytes 12582916

commit v3 on v2

--- a/solution.py
+++ b/solution.py
@@ -11,21 +11,18 @@
 RIDGE = 0.1
 LANE = 128
 STEP = 256
-SUBS = 2
-HALF = 8
+SUBS = WIN // STEP
+HALF = 16
 TAIL = WIN // LANE + 1
 MESH = pl.DeviceIdType.MESH
 
 
-def pack_kernel(body, count_ref, own_ref, market_ref, mask_ref,
-                packed_ref, own_xw_ref, packed_xw_ref, spare_ref, tile_ref):
+def pack_kernel(body, count_ref, own_ref, own_x_ref, own_w_ref,
+                packed_ref, packed_xw_ref, spare_ref, tile_ref):
     count = count_ref[0]
     tiles = (count + (LANE - 1)) // LANE
     before_tail = jnp.maximum(tiles - TAIL, 0)
-    dense = market_ref.shape[0]
     half = packed_xw_ref.shape[0] // 2
-    own_xw_ref[pl.ds(0, dense), :] = market_ref[...].astype(jnp.float32)
-    own_xw_ref[pl.ds(dense, dense), :] = mask_ref[...].astype(jnp.float32)
     packed_xw_ref[...] = jnp.zeros_like(packed_xw_ref)
     tile_ref[...] = jnp.full(tile_ref.shape, count, jnp.int32)
 
@@ -34,8 +31,8 @@
         row = jnp.maximum(j, 0)
         source = pl.ds(pl.multiple_of(row * LANE, LANE), LANE)
         packed_ref[:, pl.ds(pl.multiple_of(i * LANE, LANE), LANE)] = own_ref[:, source]
-        packed_xw_ref[pl.ds(i, 1), :] = own_xw_ref[pl.ds(row, 1), :]
-        packed_xw_ref[pl.ds(half + i, 1), :] = own_xw_ref[pl.ds(dense + row, 1), :]
+        packed_xw_ref[pl.ds(i, 1), :] = own_x_ref[pl.ds(row, 1), :]
+        packed_xw_ref[pl.ds(half + i, 1), :] = own_w_ref[pl.ds(row, 1), :]
         return 0
 
     lax.fori_loop(0, body + TAIL, fill, 0)
@@ -118,8 +115,8 @@
     free_copy.wait()
 
 
-def regress_kernel(quota, body, own_ref, own_xw_ref, got_ref, got_xw_ref, free_ref, counts_ref, out_ref,
-                   facts, hot_own, hot_got, pair, align, history, small_history, carry):
+def regress_kernel(quota, body, own_ref, own_x_ref, own_w_ref, got_ref, got_xw_ref, free_ref, counts_ref, out_ref,
+                   facts, hot_own, hot_got, pair, ones, align, history, carry):
     t = pl.program_id(0)
     me = lax.axis_index("span")
     stocks, capacity = own_ref.shape
@@ -155,9 +152,7 @@
         col = lax.broadcasted_iota(jnp.int32, (STEP, STEP), 1)
         pair[pl.ds(0, STEP), :] = jnp.where(k <= col, 1.0, 0.0).astype(bf16)
         pair[pl.ds(STEP, STEP), :] = jnp.where(k <= col, -1.0, 0.0).astype(bf16)
-        carry[...] = jnp.zeros_like(carry)
-        history[:, pl.ds(0, WIN)] = jnp.zeros((2 * stocks, WIN), bf16)
-        small_history[:, pl.ds(0, WIN)] = jnp.zeros((HALF, WIN), f32)
+        ones[...] = jnp.ones_like(ones)
 
     own_count = facts[0]
     count_1 = facts[1]
@@ -169,7 +164,6 @@
     tiles_2 = (count_2 + LANE - 1) // LANE
     base = (body + TAIL - tiles_1) * LANE
     free = jnp.minimum(body - jnp.maximum(tiles_1 - TAIL, 0), TAIL) * LANE
-    dense = own_xw_ref.shape[0] // 2
     half = got_xw_ref.shape[0] // 2
     half_free = free_ref.shape[0] // 2
 
@@ -182,7 +176,7 @@
 
     def load_own(tile):
         y = own_ref[:, pl.ds(pl.multiple_of(tile * LANE, LANE), width)]
-        return lift(y, wide(own_xw_ref, tile, width // LANE), wide(own_xw_ref, dense + tile, width // LANE))
+        return lift(y, wide(own_x_ref, tile, width // LANE), wide(own_w_ref, tile, width // LANE))
 
     def load_got(tile):
         y = got_ref[:, pl.ds(pl.multiple_of(tile * LANE, LANE), width)]
@@ -191,21 +185,32 @@
     def dot(a, b):
         return jnp.dot(a, b, preferred_element_type=f32)
 
+    def plan(first, length, offset, low, high, total):
+        head = first - offset
+        floor = (head + columns) // LANE - columns // LANE
+        reach = length + LANE
+        tile = jnp.clip(floor, 0, (total - reach) // LANE)
+        inside = (low <= head) & (head + length <= high) & (tile == floor)
+        touched = jnp.maximum(low, head) < jnp.minimum(high, head + length)
+        at = tile * LANE
+        return inside, touched, tile, (low - at, high - at, head - at)
+
+    def plan_own(first, length):
+        return plan(first, length, start, 0, own_count, capacity)
+
+    def plan_got(first, length):
+        return plan(first, length, start_1 - base, jnp.maximum(base, 0), base + count_1, columns)
+
+    def gather_all(load, tile, hot):
+        pieces = jnp.concatenate([load(tile + s * (STEP // LANE)) for s in range(SUBS)], 0)
+        result = dot(pieces, hot)
+        for s in range(SUBS):
+            align[s] = result[s * (stocks + 16):(s + 1) * (stocks + 16)]
+
     def gather(s):
-        first = t * (SUBS * STEP) + s * STEP
-
-        def plan(offset, low, high, total):
-            head = first - offset
-            floor = (head + columns) // LANE - columns // LANE
-            tile = jnp.clip(floor, 0, (total - width) // LANE)
-            inside = (low <= head) & (head + STEP <= high) & (tile == floor)
-            touched = jnp.maximum(low, head) < jnp.minimum(high, head + STEP)
-            at = tile * LANE
-            return inside, touched, tile, (low - at, high - at, head - at)
-
-        own_in, own_any, own_tile, own_map = plan(start, 0, own_count, capacity)
-        got_in, got_any, got_tile, got_map = plan(
-            start_1 - base, jnp.maximum(base, 0), base + count_1, columns)
+        first = t * WIN + s * STEP
+        own_in, own_any, own_tile, own_map = plan_own(first, STEP)
+        got_in, got_any, got_tile, got_map = plan_got(first, STEP)
 
         @pl.when(own_in)
         def _():
@@ -237,45 +242,64 @@
                 align[s] += dot(lift(got_ref[:, pl.ds(0, TAIL * LANE)], wide(free_ref, 0, TAIL),
                                      wide(free_ref, half_free, TAIL)), hot)
 
+    all_own, _, all_own_tile, _ = plan_own(t * WIN, WIN)
+    all_got, _, all_got_tile, _ = plan_got(t * WIN, WIN)
+
+    @pl.when(all_own)
+    def _():
+        gather_all(load_own, all_own_tile, hot_own[...])
+
+    @pl.when(all_got)
+    def _():
+        gather_all(load_got, all_got_tile, hot_got[...])
+
+    @pl.when(jnp.logical_not(all_own | all_got))
+    def _():
+        for s in range(SUBS):
+            gather(s)
+
+    now = lax.rem(t, 2)
+    old = 1 - now
+    small_rows = lax.broadcasted_iota(jnp.int32, (HALF, STEP), 0)
     for s in range(SUBS):
-        gather(s)
-
-    small_rows = lax.broadcasted_iota(jnp.int32, (HALF, STEP), 0)
-    moments = []
-    both = pair[...]
-    for s in range(SUBS):
-        q = pl.multiple_of(t * (SUBS * STEP) + s * STEP, STEP)
-        now_at = pl.ds(q + WIN, STEP)
-        old_at = pl.ds(q, STEP)
+        at = slice(s * STEP, (s + 1) * STEP)
         w = align[s, stocks + 1:stocks + 2, :]
         x = align[s, stocks:stocks + 1, :] * w
         y = align[s, 0:stocks, :] * w
-        cross = (x * y).astype(bf16)
-        y = y.astype(bf16)
         square = (x * x).astype(bf16).astype(f32)
         small = jnp.where(small_rows == 0, w, jnp.where(small_rows == 1, x, square))
-        parts = []
-        history[pl.ds(0, stocks), now_at] = cross
-        history[pl.ds(stocks, stocks), now_at] = y
-        small_history[:, now_at] = small
-        pieces = (
-            (0, stocks, cross, history[pl.ds(0, stocks), old_at]),
-            (stocks, stocks, y, history[pl.ds(stocks, stocks), old_at]),
-            (2 * stocks, HALF, small.astype(bf16), small_history[:, old_at].astype(bf16)),
-        )
-        for lo, size, now, old in pieces:
-            change = dot(jnp.concatenate([now, old], 1), both)
+        history[now, 0:stocks, at] = (x * y).astype(bf16)
+        history[now, stocks:2 * stocks, at] = y.astype(bf16)
+        history[now, 2 * stocks:2 * stocks + HALF, at] = small.astype(bf16)
+
+    @pl.when(t == 0)
+    def _():
+        carry[...] = dot(history[now], ones[...])
+
+    @pl.when(t > 0)
+    def _():
+        total = 2 * stocks + HALF
+        pieces = jnp.concatenate([
+            jnp.concatenate([history[now, :, s * STEP:(s + 1) * STEP], history[old, :, s * STEP:(s + 1) * STEP]], 1)
+            for s in range(SUBS)], 0)
+        change = dot(pieces, pair[...])
+
+        def summed(s, lo, size):
             rows = pl.ds(lo, size)
-            held = carry[rows, :]
-            result = change + jnp.concatenate([held] * (STEP // LANE), 1)
+            result = change[s * total + lo:s * total + lo + size] + jnp.concatenate(
+                [carry[rows, :]] * (STEP // LANE), 1)
             carry[rows, :] = jnp.broadcast_to(result[:, STEP - 1:], (size, LANE))
-            parts.append(result)
-        sum_xy, sum_y, tiny = parts
-        sum_w = tiny[0:1]
-        sum_x = tiny[1:2]
-        sum_xx = tiny[2:3]
-        inverse = 1.0 / (sum_w * sum_xx - sum_x * sum_x + RIDGE * WIN * WIN)
-        out_ref[:, s * STEP:(s + 1) * STEP] = (sum_w * inverse) * sum_xy - (sum_x * inverse) * sum_y
+            return result
+
+        for s in range(SUBS):
+            tiny = summed(s, 2 * stocks, HALF)
+            sum_w = tiny[0:1]
+            sum_x = tiny[1:2]
+            sum_xx = tiny[2:3]
+            inverse = 1.0 / (sum_w * sum_xx - sum_x * sum_x + RIDGE * WIN * WIN)
+            sum_xy = summed(s, 0, stocks)
+            sum_y = summed(s, stocks, stocks)
+            out_ref[:, s * STEP:(s + 1) * STEP] = (sum_w * inverse) * sum_xy - (sum_x * inverse) * sum_y
 
 
 def per_device(n, returns, market, mask, counts):
@@ -290,15 +314,17 @@
     half_free = -(-TAIL // 8) * 8
     shape = jax.ShapeDtypeStruct
     vmem = pl.BlockSpec(memory_space=pltpu.VMEM)
-    packed, own_xw, packed_xw, spare, count_tile = pl.pallas_call(
+    own_x = market.reshape(dense, LANE).astype(f32)
+    own_w = mask.reshape(dense, LANE).astype(f32)
+    packed, packed_xw, spare, count_tile = pl.pallas_call(
         functools.partial(pack_kernel, body),
-        out_shape=(shape((stocks, columns), bf16), shape((2 * dense, LANE), f32), shape((2 * half, LANE), f32),
+        out_shape=(shape((stocks, columns), bf16), shape((2 * half, LANE), f32),
                    shape((8, TAIL * LANE), f32), shape((8, LANE), i32)),
         in_specs=[pl.BlockSpec(memory_space=pltpu.SMEM), vmem, vmem, vmem],
-        out_specs=(vmem,) * 5,
+        out_specs=(vmem,) * 4,
         compiler_params=pltpu.CompilerParams(vmem_limit_bytes=16 * 2**20),
         name="pack",
-    )(counts, returns, market.reshape(dense, LANE), mask.reshape(dense, LANE))
+    )(counts, returns, own_x, own_w)
     got, got_xw, got_free, gathered = pl.pallas_call(
         functools.partial(exchange_kernel, n, body),
         out_shape=(shape((stocks, columns), bf16), shape((2 * half, LANE), f32),
@@ -323,21 +349,21 @@
         functools.partial(regress_kernel, quota, body),
         out_shape=shape((stocks, quota), f32),
         grid=(steps,),
-        in_specs=[vmem] * 6,
+        in_specs=[vmem] * 7,
         out_specs=pl.BlockSpec((stocks, SUBS * STEP), lambda t: (0, jnp.maximum(t - lag, 0))),
         scratch_shapes=[
             pltpu.SMEM((4,), i32),
             pltpu.VMEM((STEP + LANE, STEP), bf16),
             pltpu.VMEM((STEP + LANE, STEP), bf16),
             pltpu.VMEM((2 * STEP, STEP), bf16),
+            pltpu.VMEM((WIN, LANE), bf16),
             pltpu.VMEM((SUBS, stocks + 16, STEP), f32),
-            pltpu.VMEM((2 * stocks, quota + 2 * WIN), bf16),
-            pltpu.VMEM((HALF, quota + 2 * WIN), f32),
+            pltpu.VMEM((2, 2 * stocks + HALF, WIN), bf16),
             pltpu.VMEM((2 * stocks + HALF, LANE), f32),
         ],
         compiler_params=pltpu.CompilerParams(vmem_limit_bytes=32 * 2**20),
         name="regress",
-    )(returns, own_xw, got, got_xw, got_free, gathered)
+    )(returns, own_x, own_w, got, got_xw, got_free, gathered)
 
 
 def solution(mesh):

time: 62.1 us -> 58.4 us (0.940)
  Pallas kernels: 57.5 us -> 53.8 us
  other arithmetic: 0 us -> 1.48 us
  local copies, waits for them, and re-layouts: 3.66 us -> 2.19 us
    pallas_call x1, Pallas kernels: 15 us -> 11.3 us  [per_device(): pl.pallas_call(functools.partial(regress_kernel, quota, body), out_shape=...]
    convert_element_type x0 -> x2, other arithmetic: none -> 1.48 us  [the longest x1 0.76 us: per_device(): own_w = mask.reshape(dense, LANE).astype(f32)]
    unnamed x8 -> x4, local copies, waits for them, and re-layouts: 3.66 us -> 2.19 us
where the time goes in v3:
time: 58.4 us; the launch traced here: 58.1 us
  Pallas kernels  53.8 us (92%)
  local copies, waits for them, and re-layouts  2.19 us (4%)
  other arithmetic  1.48 us (3%)
  between operations  0.68 us (1%)
    pallas_call x1, Pallas kernels, per_device(): pl.pallas_call(functools.partial(exchange_kernel, n, body), out_shape=(sh...  41.5 us
    pallas_call x1, Pallas kernels, per_device(): pl.pallas_call(functools.partial(regress_kernel, quota, body), out_shape=...  11.3 us
    unnamed x4, local copies, waits for them, and re-layouts  2.19 us

profile of v3, /device:TPU:0, one launch (start us, length us, event | category | flops | bytes accessed | tf_op | source)
XLA Modules:
  0.0 58.1 jit_solution(15114143896440370485)
XLA Ops:
  0.7 0.7 %bitcast_convert_fusion.own_x_ref = f32[64,128]{1,0:T(8,128)S(1)} fusion(bf16[8192]{0:T(1024)(128)(2,1)} %param.5), kind=kLoop, calls=%fused_computation.1 | loop fusion | flops 8192 | bytes 49152 | tf_op jit(solution)/shard_map/convert_element_type | solution.py:317
  1.4 0.8 %convert_bitcast_fusion.own_w_ref = f32[64,128]{1,0:T(8,128)S(1)} fusion(s32[8192]{0:T(1024)} %param.6), kind=kLoop, calls=%fused_computation | loop fusion | flops 8192 | bytes 65536 | tf_op jit(solution)/shard_map/convert_element_type | solution.py:318
  2.1 0.0 copy-start
  2.1 2.2 %copy-done = bf16[256,8192]{1,0:T(8,128)(2,1)S(1)} copy-done((bf16[256,8192]{1,0:T(8,128)(2,1)S(1)}, bf16[256,8192]{1,0:T(8,128)(2,1)}, u32[]{:S(2)}) %copy-start) | copy-done | bytes 4194328
  4.3 0.0 copy-start.1
  4.3 1.0 %pack.1 = (bf16[256,5376]{1,0:T(8,128)(2,1)S(1)}, f32[96,128]{1,0:T(8,128)S(1)}, f32[8,1152]{1,0:T(8,128)S(1)}, s32[8,128]{1,0:T(8,128)S(1)}) custom-call(s32[1]{0:T(128)S(6)} %copy.5.count_ref, bf16[256,8192]{1,0:T(8,128)(2,1)S(1)} %copy-done, f32[64,128]{1,0:T(8,128)S(1)} %bitcast_convert_fusion.own_x_ref, f32[64,128]{1,0:T(8,128)S(1)} %convert_bitcast_fusion.own_w_ref), custom_call_target="tpu_custom_call" | custom-call | tf_op jit(solution)/shard_map/pack/pallas_call | solution.py:319
  5.4 41.5 %exchange.1 = (bf16[256,5376]{1,0:T(8,128)(2,1)S(1)}, f32[96,128]{1,0:T(8,128)S(1)}, f32[32,128]{1,0:T(8,128)S(1)}, s32[32,8,128]{2,1,0:T(8,128)S(1)}) custom-call(bf16[256,5376]{1,0:T(8,128)(2,1)S(1)} %get-tuple-element.13.packed_ref, f32[96,128]{1,0:T(8,128)S(1)} %get-tuple-element.14.packed_xw_ref, f32[8,1152]{1,0:T(8,128)S(1)} %get-tuple-element.15.spare_ref, ...), custom_call_target="tpu_custom_call" | custom-call | tf_op jit(solution)/shard_map/exchange/pallas_call | solution.py:328
  46.9 0.0 copy-done.1
  46.9 11.3 %regress.1 = f32[256,4096]{1,0:T(8,128)} custom-call(bf16[256,8192]{1,0:T(8,128)(2,1)S(1)} %copy-done.1, f32[64,128]{1,0:T(8,128)S(1)} %bitcast_convert_fusion.own_x_ref, f32[64,128]{1,0:T(8,128)S(1)} %convert_bitcast_fusion.own_w_ref, bf16[256,5376]{1,0:T(8,128)(2,1)S(1)} %get-tuple-element.17.got_ref, f32[96,128]{1,0:T(8,128)S(1)} %get-tuple-element.18.got_xw_ref, ...), custom_call_target="tpu_custom_call" | custom-call | tf_op jit(solution)/shard_map/regress/pallas_call | solution.py:348
Async XLA Ops:
  2.1 2.2 %copy-start = (bf16[256,8192]{1,0:T(8,128)(2,1)S(1)}, bf16[256,8192]{1,0:T(8,128)(2,1)}, u32[]{:S(2)}) copy-start(bf16[256,8192]{1,0:T(8,128)(2,1)} %own_ref.3) | copy-start | bytes 12582916
  4.3 42.5 %copy-start.1 = (bf16[256,8192]{1,0:T(8,128)(2,1)S(1)}, bf16[256,8192]{1,0:T(8,128)(2,1)}, u32[]{:S(2)}) copy-start(bf16[256,8192]{1,0:T(8,128)(2,1)} %own_ref.3) | copy-start | bytes 12582916
